TPU v7x, 256 devices: a whole 4x4x8 slice. The times are simulated.
256 devices in a mesh: row: 16 (over z, core), col: 16 (over y, x).
Axes of the slice: x: 4, y: 4, z: 8, core: 2. Of those that a mesh axis runs over, the one named last changes fastest.
Arguments:
- design: float32 [8192, 65536], P('row', 'col'), may hold values from -0.0625 to 0.0625
- targets: float32 [32, 8192], P(None, 'row'), may hold values from -6 to 6
- warm_solution: float32 [32, 65536], P(None, ('col', 'row')), may hold values from -2 to 2
- warm_sparse: float32 [32, 65536], P(None, ('col', 'row')), may hold values from -2 to 2
- warm_dual: float32 [32, 65536], P(None, ('col', 'row')), may hold values from -1.5 to 1.5
- sparsity: float32 [32], replicated, may hold values from 0.02 to 0.2
Outputs:
- solution: float32 [32, 65536], P(None, ('col', 'row'))
- sparse: float32 [32, 65536], P(None, ('col', 'row'))
- scaled_dual: float32 [32, 65536], P(None, ('col', 'row'))
All inputs are finite; a program needn't handle non-finite values.
Results may differ from a plain program's by a relative error of at most 0.0003.
Values sent between devices are 32-bit elements; how exact they have to be, the bound alone decides.
No kernel may reach another device: no remote copies, remote signals or barrier semaphores. Data moves between devices by JAX's collectives and lax.ppermute only.
A program may use at most 64 MiB of HBM per device.

v0:
```python
import jax
import jax.numpy as jnp
from jax import lax
from jax.sharding import Mesh
from jax.sharding import PartitionSpec as P

STEPS = 3
COL = ("col_0", "col_1")
ROW = ("row_0", "row_1")
ROW_COL = ("row_0", "row_1", "col_0", "col_1")
COL_ROW = ("col_0", "col_1", "row_0", "row_1")
penalty = 0.5


def sent_to_all(array, axis):
    peers = lax.axis_size(axis)
    return lax.all_to_all(
        jnp.broadcast_to(array[None], (peers, *array.shape)), axis, 0, 0, tiled=True
    )


def taken_together(array, axis):
    everything = sent_to_all(array, axis)
    return jnp.sum(everything, axis=0)


def split_up(array, dim, peers):
    before, after = (array.shape[:dim], array.shape[dim + 1 :])
    return jnp.moveaxis(array.reshape(*before, peers, -1, *after), dim, 0)


def summed_on_arrival(array, axis, dim):
    peers = lax.axis_size(axis)
    tiles = lax.all_to_all(split_up(array, dim, peers), axis, 0, 0, tiled=True)
    return jnp.sum(tiles, axis=0)


def by_axis(array, axes):
    for axis in axes:
        array = lax.psum(array, axis)
    return array


def forward_part(vector, block):
    return lax.dot_general(
        vector,
        block,
        (((1,), (1,)), ((), ())),
        precision=lax.Precision.HIGHEST,
        preferred_element_type=jnp.float32,
    )


def backward_part(values, design):
    return jnp.dot(
        values, design, precision=lax.Precision.HIGHEST, preferred_element_type=jnp.float32
    )


def row_sums(values):
    return jnp.sum(values, axis=1, keepdims=True)


def on_device(design, targets, warm_solution, warm_sparse, warm_dual, sparsity):

    def rows_total(partial_value):
        return taken_together(partial_value, COL)

    def spread(vector):
        return rows_total(forward_part(lax.all_gather(vector, ROW, axis=1, tiled=True), design))

    def collect(values):
        return summed_on_arrival(backward_part(values, design), ROW, 1)

    def total(stats):
        return jax.tree.map(lambda part: by_axis(part, ROW_COL), stats)

    solution, sparse, scaled_dual = (warm_solution, warm_sparse, warm_dual)

    def gram(vector):
        return collect(spread(vector)) + penalty * vector

    thresh = (sparsity / penalty)[:, None]
    residual = collect(targets - spread(solution)) + penalty * (sparse - scaled_dual - solution)
    image = gram(residual)
    norm_now, product = total((row_sums(residual * residual), row_sums(residual * image)))
    alpha = norm_now / product
    direction = residual
    along = image
    for step in range(STEPS):
        solution = solution + alpha * direction
        residual = residual - alpha * along
        if step + 1 < STEPS:
            image = gram(residual)
            norm_next, product = total((row_sums(residual * residual), row_sums(residual * image)))
            ratio = norm_next / norm_now
            alpha = norm_next / (product - ratio * norm_next / alpha)
            direction = residual + ratio * direction
            along = image + ratio * along
            norm_now = norm_next
    merged = solution + scaled_dual
    sparse = jnp.sign(merged) * jnp.maximum(jnp.abs(merged) - thresh, 0.0)
    scaled_dual = merged - sparse
    return (solution, sparse, scaled_dual)


def solution(mesh):
    finer = Mesh(mesh.devices.reshape(8, 2, 4, 4), ("row_0", "row_1", "col_0", "col_1"))
    return jax.shard_map(
        on_device,
        mesh=finer,
        in_specs=(
            P(ROW, COL),
            P(None, ROW),
            P(None, COL_ROW),
            P(None, COL_ROW),
            P(None, COL_ROW),
            P(),
        ),
        out_specs=(P(None, COL_ROW), P(None, COL_ROW), P(None, COL_ROW)),
        check_vma=False,
    )
```

profile of v0, /device:TPU:2, one launch (start us, length us, event | category | flops | bytes accessed | tf_op | source)
XLA Modules:
  0.0 428.4 jit_solution(11205787050152184294)
XLA Ops:
  0.6 21.7 %all_gather.12 = f32[32,4096]{1,0:T(8,128)S(1)} all-gather(f32[32,256]{1,0:T(8,128)} %param.8), channel_id=1, replica_groups=mesh['row_0'=8,'row_1'=2,'col_0'=4,'col_1'=4] {'row_0','row_1'}, dimensions={1}, use_global_device_ids=true | all-gather | bytes 557056 | tf_op jit(solution)/shard_map/all_gather | solution.py:70
  22.3 9.7 %fusion.8 = f32[32,512]{1,0:T(8,128)S(1)} fusion(f32[32,4096]{1,0:T(8,128)S(1)} %all_gather.12, f32[512,4096]{1,0:T(8,128)} %param.6), kind=kOutput, calls=%fused_computation.30 | convolution fusion | flops 805306368 | bytes 8978432 | tf_op jit(solution)/shard_map/dot_general | solution.py:45
  32.2 23.6 %all_to_all.40 = f32[16,32,512]{2,1,0:T(8,128)S(1)} all-to-all(f32[16,32,512]{2,1,0:T(8,128)S(1)} %broadcast_in_dim.20), channel_id=1, replica_groups=mesh['row_0'=8,'row_1'=2,'col_0'=4,'col_1'=4] {'col_0','col_1'}, dimensions={0} | all-to-all | bytes 2097152 | tf_op jit(solution)/shard_map/all_to_all | solution.py:17
  63.1 19.5 %all_to_all.41 = f32[16,32,256]{2,1,0:T(8,128)S(1)} all-to-all(f32[16,32,256]{2,1,0:T(8,128)S(1)} %bitcast.55), channel_id=1, replica_groups=mesh['row_0'=8,'row_1'=2,'col_0'=4,'col_1'=4] {'row_0','row_1'}, dimensions={0} | all-to-all | bytes 1048576 | tf_op jit(solution)/shard_map/all_to_all | solution.py:34
  82.7 17.2 %all_gather.13 = f32[32,4096]{1,0:T(8,128)S(1)} all-gather(f32[32,256]{1,0:T(8,128)S(1)} %multiply_add_fusion.3), channel_id=1, replica_groups=mesh['row_0'=8,'row_1'=2,'col_0'=4,'col_1'=4] {'row_0','row_1'}, dimensions={1}, use_global_device_ids=true | all-gather | bytes 557056 | tf_op jit(solution)/shard_map/all_gather | solution.py:70
  99.9 9.7 %fusion.9 = f32[32,512]{1,0:T(8,128)S(1)} fusion(f32[32,4096]{1,0:T(8,128)S(1)} %all_gather.13, f32[512,4096]{1,0:T(8,128)} %param.6), kind=kOutput, calls=%fused_computation.31 | convolution fusion | flops 805306368 | bytes 8978432 | tf_op jit(solution)/shard_map/dot_general | solution.py:45
  132.5 9.9 %convolution_bitcast_fusion.2 = f32[16,32,256]{2,1,0:T(8,128)S(1)} fusion(f32[16,256,512]{2,1,0:T(8,128)} %bitcast.51, f32[32,512]{1,0:T(8,128)S(1)} %reduce_sum.129), kind=kOutput, calls=%fused_computation.2 | convolution fusion | flops 805306368 | bytes 8978432 | tf_op jit(solution)/shard_map/dot_general | solution.py:55
  142.4 20.9 %all_to_all.42 = f32[16,32,256]{2,1,0:T(8,128)S(1)} all-to-all(f32[16,32,256]{2,1,0:T(8,128)S(1)} %convolution_bitcast_fusion.2), channel_id=1, replica_groups=mesh['row_0'=8,'row_1'=2,'col_0'=4,'col_1'=4] {'row_0','row_1'}, dimensions={0} | all-to-all | bytes 1048576 | tf_op jit(solution)/shard_map/all_to_all | solution.py:34
  163.4 14.9 %all-reduce.2 = (f32[32,1]{0,1:T(1,128)S(1)}, f32[32,1]{0,1:T(1,128)S(1)}) all-reduce(f32[32,1]{0,1:T(1,128)S(1)} %bitcast.62, f32[32,1]{0,1:T(1,128)S(1)} %bitcast.61), channel_id=1, replica_groups=mesh['row_0'=8,'row_1'=2,'col_0'=4,'col_1'=4] {'row_0'}, use_global_device_ids=true, to_apply=%region_3.0 | all-reduce | flops 64 | bytes 512 | tf_op jit(solution)/shard_map/psum | solution.py:40
  189.8 10.1 %all-reduce.5 = (f32[32,1]{0,1:T(1,128)S(1)}, f32[32,1]{0,1:T(1,128)S(1)}) all-reduce(f32[32,1]{0,1:T(1,128)S(1)} %get-tuple-element.25, f32[32,1]{0,1:T(1,128)S(1)} %get-tuple-element.26), channel_id=1, replica_groups=mesh['row_0'=8,'row_1'=2,'col_0'=4,'col_1'=4] {'col_1'}, use_global_device_ids=true, to_apply=%region_6.0 | all-reduce | flops 64 | bytes 512 | tf_op jit(solution)/shard_map/psum | solution.py:40
  200.0 16.8 %all_gather.14 = f32[32,4096]{1,0:T(8,128)S(1)} all-gather(f32[32,256]{1,0:T(8,128)S(1)} %multiply_subtract_fusion.1), channel_id=1, replica_groups=mesh['row_0'=8,'row_1'=2,'col_0'=4,'col_1'=4] {'row_0','row_1'}, dimensions={1}, use_global_device_ids=true | all-gather | bytes 557056 | tf_op jit(solution)/shard_map/all_gather | solution.py:70
  216.9 9.7 %fusion.10 = f32[32,512]{1,0:T(8,128)S(1)} fusion(f32[32,4096]{1,0:T(8,128)S(1)} %all_gather.14, f32[512,4096]{1,0:T(8,128)} %param.6), kind=kOutput, calls=%fused_computation.32 | convolution fusion | flops 805306368 | bytes 8978432 | tf_op jit(solution)/shard_map/dot_general | solution.py:45
  226.7 19.7 %all_to_all.43 = f32[16,32,512]{2,1,0:T(8,128)S(1)} all-to-all(f32[16,32,512]{2,1,0:T(8,128)S(1)} %broadcast_in_dim.48), channel_id=1, replica_groups=mesh['row_0'=8,'row_1'=2,'col_0'=4,'col_1'=4] {'col_0','col_1'}, dimensions={0} | all-to-all | bytes 2097152 | tf_op jit(solution)/shard_map/all_to_all | solution.py:17
  246.5 9.9 %convolution_bitcast_fusion.1 = f32[16,32,256]{2,1,0:T(8,128)S(1)} fusion(f32[16,256,512]{2,1,0:T(8,128)} %bitcast.52, f32[32,512]{1,0:T(8,128)S(1)} %reduce_sum.133), kind=kOutput, calls=%fused_computation.1 | convolution fusion | flops 805306368 | bytes 8978432 | tf_op jit(solution)/shard_map/dot_general | solution.py:55
  256.4 21.1 %all_to_all.44 = f32[16,32,256]{2,1,0:T(8,128)S(1)} all-to-all(f32[16,32,256]{2,1,0:T(8,128)S(1)} %convolution_bitcast_fusion.1), channel_id=1, replica_groups=mesh['row_0'=8,'row_1'=2,'col_0'=4,'col_1'=4] {'row_0','row_1'}, dimensions={0} | all-to-all | bytes 1048576 | tf_op jit(solution)/shard_map/all_to_all | solution.py:34
  277.7 14.9 %all-reduce.1 = (f32[32,1]{0,1:T(1,128)S(1)}, f32[32,1]{0,1:T(1,128)S(1)}) all-reduce(f32[32,1]{0,1:T(1,128)S(1)} %bitcast.64, f32[32,1]{0,1:T(1,128)S(1)} %bitcast.63), channel_id=1, replica_groups=mesh['row_0'=8,'row_1'=2,'col_0'=4,'col_1'=4] {'row_0'}, use_global_device_ids=true, to_apply=%region_15.0 | all-reduce | flops 64 | bytes 512 | tf_op jit(solution)/shard_map/psum | solution.py:40
  303.6 9.1 %all-reduce.4 = (f32[32,1]{0,1:T(1,128)S(1)}, f32[32,1]{0,1:T(1,128)S(1)}) all-reduce(f32[32,1]{0,1:T(1,128)S(1)} %get-tuple-element.23, f32[32,1]{0,1:T(1,128)S(1)} %get-tuple-element.24), channel_id=1, replica_groups=mesh['row_0'=8,'row_1'=2,'col_0'=4,'col_1'=4] {'col_1'}, use_global_device_ids=true, to_apply=%region_18.0 | all-reduce | flops 64 | bytes 512 | tf_op jit(solution)/shard_map/psum | solution.py:40
  312.8 17.0 %all_gather.15 = f32[32,4096]{1,0:T(8,128)S(1)} all-gather(f32[32,256]{1,0:T(8,128)S(1)} %multiply_subtract_fusion), channel_id=1, replica_groups=mesh['row_0'=8,'row_1'=2,'col_0'=4,'col_1'=4] {'row_0','row_1'}, dimensions={1}, use_global_device_ids=true | all-gather | bytes 557056 | tf_op jit(solution)/shard_map/all_gather | solution.py:70
  329.8 9.7 %fusion.11 = f32[32,512]{1,0:T(8,128)S(1)} fusion(f32[32,4096]{1,0:T(8,128)S(1)} %all_gather.15, f32[512,4096]{1,0:T(8,128)} %param.6), kind=kOutput, calls=%fused_computation.33 | convolution fusion | flops 805306368 | bytes 8978432 | tf_op jit(solution)/shard_map/dot_general | solution.py:45
  339.7 20.1 %all_to_all.45 = f32[16,32,512]{2,1,0:T(8,128)S(1)} all-to-all(f32[16,32,512]{2,1,0:T(8,128)S(1)} %broadcast_in_dim.51), channel_id=1, replica_groups=mesh['row_0'=8,'row_1'=2,'col_0'=4,'col_1'=4] {'col_0','col_1'}, dimensions={0} | all-to-all | bytes 2097152 | tf_op jit(solution)/shard_map/all_to_all | solution.py:17
  359.8 10.7 %convolution_bitcast_fusion = f32[16,32,256]{2,1,0:T(8,128)} fusion(f32[16,256,512]{2,1,0:T(8,128)} %bitcast.53, f32[32,512]{1,0:T(8,128)S(1)} %reduce_sum.137), kind=kOutput, calls=%fused_computation | convolution fusion | flops 805306368 | bytes 8978432 | tf_op jit(solution)/shard_map/dot_general | solution.py:55
  375.9 15.9 %all-to-all-done.7 = f32[16,32,256]{2,1,0:T(8,128)S(1)} async-done(((f32[16,32,256]{2,1,0:T(8,128)}), f32[16,32,256]{2,1,0:T(8,128)S(1)}, u32[]{:S(2)}, u32[]{:S(2)}) %all-to-all-start.7) | async-done | bytes 524320 | tf_op jit(solution)/shard_map/all_to_all | solution.py:34
  392.0 14.9 %all-reduce = (f32[32,1]{0,1:T(1,128)S(1)}, f32[32,1]{0,1:T(1,128)S(1)}) all-reduce(f32[32,1]{0,1:T(1,128)S(1)} %bitcast.60, f32[32,1]{0,1:T(1,128)S(1)} %bitcast.59), channel_id=1, replica_groups=mesh['row_0'=8,'row_1'=2,'col_0'=4,'col_1'=4] {'row_0'}, use_global_device_ids=true, to_apply=%region_27.0 | all-reduce | flops 64 | bytes 512 | tf_op jit(solution)/shard_map/psum | solution.py:40
  417.9 9.1 %all-reduce.3 = (f32[32,1]{0,1:T(1,128)S(1)}, f32[32,1]{0,1:T(1,128)S(1)}) all-reduce(f32[32,1]{0,1:T(1,128)S(1)} %get-tuple-element.21, f32[32,1]{0,1:T(1,128)S(1)} %get-tuple-element.22), channel_id=1, replica_groups=mesh['row_0'=8,'row_1'=2,'col_0'=4,'col_1'=4] {'col_1'}, use_global_device_ids=true, to_apply=%region_30.0 | all-reduce | flops 64 | bytes 512 | tf_op jit(solution)/shard_map/psum | solution.py:40
  (46 shorter events, 71.6 us)
Async XLA Ops:
  0.6 55.2 %copy-start.2 = (f32[32,512]{1,0:T(8,128)S(1)}, f32[32,512]{1,0:T(8,128)}, u32[]{:S(2)}) copy-start(f32[32,512]{1,0:T(8,128)} %param.7) | copy-start | bytes 196612
  32.0 50.6 %copy-start = (f32[32,256]{1,0:T(8,128)S(1)}, f32[32,256]{1,0:T(8,128)}, u32[]{:S(2)}) copy-start(f32[32,256]{1,0:T(8,128)} %param.8) | copy-start | bytes 98308
  32.0 50.6 %copy-start.1 = (f32[32,256]{1,0:T(8,128)S(1)}, f32[32,256]{1,0:T(8,128)}, u32[]{:S(2)}) copy-start(f32[32,256]{1,0:T(8,128)} %param.10) | copy-start | bytes 98308
  32.0 50.6 %copy-start.3 = (f32[32,256]{1,0:T(8,128)S(1)}, f32[32,256]{1,0:T(8,128)}, u32[]{:S(2)}) copy-start(f32[32,256]{1,0:T(8,128)} %param.9) | copy-start | bytes 98308
  110.8 21.6 %all-to-all-start.2 = ((f32[16,32,512]{2,1,0:T(8,128)}), f32[16,32,512]{2,1,0:T(8,128)S(1)}, u32[]{:S(2)}, u32[]{:S(2)}) async-start(f32[16,32,512]{2,1,0:T(8,128)} %broadcast_in_dim.22), calls=%async_computation.2 | async-start | bytes 2097152 | tf_op jit(solution)/shard_map/all_to_all | solution.py:17
  339.6 36.3 %copy-start.4 = (f32[32]{0:T(128)S(1)}, f32[32]{0:T(128)}, u32[]{:S(2)}) copy-start(f32[32]{0:T(128)} %param.11) | copy-start | bytes 388
  370.5 21.3 %all-to-all-start.7 = ((f32[16,32,256]{2,1,0:T(8,128)}), f32[16,32,256]{2,1,0:T(8,128)S(1)}, u32[]{:S(2)}, u32[]{:S(2)}) async-start(f32[16,32,256]{2,1,0:T(8,128)} %convolution_bitcast_fusion), calls=%async_computation.7 | async-start | bytes 1048576 | tf_op jit(solution)/shard_map/all_to_all | solution.py:34
where the time goes:
time: 429 us; the launch traced here: 428 us
  blocking collectives  304 us (71%)
  matrix products  76.5 us (18%)
  waiting for transfers between devices  23.6 us (6%)
  local copies, waits for them, and re-layouts  10.6 us (2%)
  starting transfers between devices  10.2 us (2%)
    psum x12, blocking collectives, by_axis(): array = lax.psum(array, axis)  107 us
    all_gather x4, blocking collectives, spread(): lax.all_gather(vector, ROW, axis=1, tiled=True)  72.8 us
    all_to_all x3, blocking collectives, sent_to_all(): lax.all_to_all(jnp.broadcast_to(array[None], (peers, *array.shape)), axis...  63.4 us
    all_to_all x3, blocking collectives, summed_on_arrival(): tiles = lax.all_to_all(split_up(array, dim, peers), axis, 0, 0, tiled=True)  61.4 us
    dot_general x4, matrix products, forward_part(): lax.dot_general(vector, block, (((1,), (1,)), ((), ())), precision=lax.Pr...  38.9 us
    dot_general x4, matrix products, backward_part(): jnp.dot(values, design, precision=lax.Precision.HIGHEST, preferred_elemen...  37.6 us
    all_to_all x1, waiting for transfers between devices, summed_on_arrival(): tiles = lax.all_to_all(split_up(array, dim, peers), axis, 0, 0, tiled=True)  15.9 us
    dot_general x1, local copies, waits for them, and re-layouts, backward_part(): jnp.dot(values, design, precision=lax.Precision.HIGHEST, preferred_elemen...  9.01 us
  transfers between devices with their start and end apart: 2, of which 2 were waited for; matrix products, arithmetic and copies ran while one was open for 2% of the time, Pallas kernels for 0%

commit v1 on v0

--- a/solution.py
+++ b/solution.py
@@ -67,7 +67,14 @@
         return taken_together(partial_value, COL)
 
     def spread(vector):
-        return rows_total(forward_part(lax.all_gather(vector, ROW, axis=1, tiled=True), design))
+        return rows_total(
+            forward_part(
+                jnp.concatenate(
+                    lax.all_to_all(jnp.stack([vector] * lax.axis_size(ROW)), ROW, 0, 0), axis=1
+                ),
+                design,
+            )
+        )
 
     def collect(values):
         return summed_on_arrival(backward_part(values, design), ROW, 1)

time: 429 us -> 443 us (1.033)
  blocking collectives: 304 us -> 318 us
    all_to_all x0 -> x4, blocking collectives: none -> 87.9 us  [spread(): lax.all_to_all(jnp.stack([vector] * lax.axis_size(ROW)), ROW, 0, 0)]
    all_gather x4 -> x0, blocking collectives: 72.8 us -> none  [spread(): lax.all_gather(vector, ROW, axis=1, tiled=True)]
where the time goes in v1:
time: 443 us; the launch traced here: 442 us
  blocking collectives  318 us (72%)
  matrix products  76.5 us (17%)
  waiting for transfers between devices  23.4 us (5%)
  local copies, waits for them, and re-layouts  11.7 us (3%)
  starting transfers between devices  8.48 us (2%)
    psum x12, blocking collectives, by_axis(): array = lax.psum(array, axis)  107 us
    all_to_all x4, blocking collectives, spread(): lax.all_to_all(jnp.stack([vector] * lax.axis_size(ROW)), ROW, 0, 0)  87.9 us
    all_to_all x3, blocking collectives, sent_to_all(): lax.all_to_all(jnp.broadcast_to(array[None], (peers, *array.shape)), axis...  64.8 us
    all_to_all x3, blocking collectives, summed_on_arrival(): tiles = lax.all_to_all(split_up(array, dim, peers), axis, 0, 0, tiled=True)  58.3 us
    dot_general x4, matrix products, forward_part(): lax.dot_general(vector, block, (((1,), (1,)), ((), ())), precision=lax.Pr...  38.9 us
    dot_general x4, matrix products, backward_part(): jnp.dot(values, design, precision=lax.Precision.HIGHEST, preferred_elemen...  37.6 us
    all_to_all x1, waiting for transfers between devices, summed_on_arrival(): tiles = lax.all_to_all(split_up(array, dim, peers), axis, 0, 0, tiled=True)  15.9 us
    dot_general x1, local copies, waits for them, and re-layouts, backward_part(): jnp.dot(values, design, precision=lax.Precision.HIGHEST, preferred_elemen...  9.01 us
  transfers between devices with their start and end apart: 2, of which 2 were waited for; matrix products, arithmetic and copies ran while one was open for 2% of the time, Pallas kernels for 0%

profile of v1, /device:TPU:2, one launch (start us, length us, event | category | flops | bytes accessed | tf_op | source)
XLA Modules:
  0.0 441.6 jit_solution(17682828404812773208)
XLA Ops:
  1.5 24.3 %all_to_all.60 = f32[16,32,256]{2,1,0:T(8,128)S(1)} all-to-all(f32[16,32,256]{2,1,0:T(8,128)S(1)} %stack.8), channel_id=1, replica_groups=mesh['row_0'=8,'row_1'=2,'col_0'=4,'col_1'=4] {'row_0','row_1'}, dimensions={0} | all-to-all | bytes 1048576 | tf_op jit(solution)/shard_map/all_to_all | solution.py:73
  25.8 9.7 %fusion.8 = f32[32,512]{1,0:T(8,128)S(1)} fusion(f32[32,4096]{1,0:T(8,128)S(1)} %bitcast.66, f32[512,4096]{1,0:T(8,128)} %param.6), kind=kOutput, calls=%fused_computation.30 | convolution fusion | flops 805306368 | bytes 8978432 | tf_op jit(solution)/shard_map/dot_general | solution.py:45
  35.7 24.1 %all_to_all.61 = f32[16,32,512]{2,1,0:T(8,128)S(1)} all-to-all(f32[16,32,512]{2,1,0:T(8,128)S(1)} %broadcast_in_dim.20), channel_id=1, replica_groups=mesh['row_0'=8,'row_1'=2,'col_0'=4,'col_1'=4] {'col_0','col_1'}, dimensions={0} | all-to-all | bytes 2097152 | tf_op jit(solution)/shard_map/all_to_all | solution.py:17
  67.1 19.2 %all_to_all.62 = f32[16,32,256]{2,1,0:T(8,128)S(1)} all-to-all(f32[16,32,256]{2,1,0:T(8,128)S(1)} %bitcast.72), channel_id=1, replica_groups=mesh['row_0'=8,'row_1'=2,'col_0'=4,'col_1'=4] {'row_0','row_1'}, dimensions={0} | all-to-all | bytes 1048576 | tf_op jit(solution)/shard_map/all_to_all | solution.py:34
  86.5 20.0 %all_to_all.63 = f32[16,32,256]{2,1,0:T(8,128)S(1)} all-to-all(f32[16,32,256]{2,1,0:T(8,128)S(1)} %stack.9), channel_id=1, replica_groups=mesh['row_0'=8,'row_1'=2,'col_0'=4,'col_1'=4] {'row_0','row_1'}, dimensions={0} | all-to-all | bytes 1048576 | tf_op jit(solution)/shard_map/all_to_all | solution.py:73
  106.5 9.7 %fusion.9 = f32[32,512]{1,0:T(8,128)S(1)} fusion(f32[32,4096]{1,0:T(8,128)S(1)} %bitcast.68, f32[512,4096]{1,0:T(8,128)} %param.6), kind=kOutput, calls=%fused_computation.31 | convolution fusion | flops 805306368 | bytes 8978432 | tf_op jit(solution)/shard_map/dot_general | solution.py:45
  139.0 9.9 %convolution_bitcast_fusion.2 = f32[16,32,256]{2,1,0:T(8,128)S(1)} fusion(f32[16,256,512]{2,1,0:T(8,128)} %bitcast.63, f32[32,512]{1,0:T(8,128)S(1)} %reduce_sum.129), kind=kOutput, calls=%fused_computation.2 | convolution fusion | flops 805306368 | bytes 8978432 | tf_op jit(solution)/shard_map/dot_general | solution.py:55
  148.9 19.8 %all_to_all.64 = f32[16,32,256]{2,1,0:T(8,128)S(1)} all-to-all(f32[16,32,256]{2,1,0:T(8,128)S(1)} %convolution_bitcast_fusion.2), channel_id=1, replica_groups=mesh['row_0'=8,'row_1'=2,'col_0'=4,'col_1'=4] {'row_0','row_1'}, dimensions={0} | all-to-all | bytes 1048576 | tf_op jit(solution)/shard_map/all_to_all | solution.py:34
  168.9 14.9 %all-reduce.2 = (f32[32,1]{0,1:T(1,128)S(1)}, f32[32,1]{0,1:T(1,128)S(1)}) all-reduce(f32[32,1]{0,1:T(1,128)S(1)} %bitcast.82, f32[32,1]{0,1:T(1,128)S(1)} %bitcast.81), channel_id=1, replica_groups=mesh['row_0'=8,'row_1'=2,'col_0'=4,'col_1'=4] {'row_0'}, use_global_device_ids=true, to_apply=%region_3.0 | all-reduce | flops 64 | bytes 512 | tf_op jit(solution)/shard_map/psum | solution.py:40
  194.9 10.8 %all-reduce.5 = (f32[32,1]{0,1:T(1,128)S(1)}, f32[32,1]{0,1:T(1,128)S(1)}) all-reduce(f32[32,1]{0,1:T(1,128)S(1)} %get-tuple-element.25, f32[32,1]{0,1:T(1,128)S(1)} %get-tuple-element.26), channel_id=1, replica_groups=mesh['row_0'=8,'row_1'=2,'col_0'=4,'col_1'=4] {'col_1'}, use_global_device_ids=true, to_apply=%region_6.0 | all-reduce | flops 64 | bytes 512 | tf_op jit(solution)/shard_map/psum | solution.py:40
  205.8 21.8 %all_to_all.65 = f32[16,32,256]{2,1,0:T(8,128)S(1)} all-to-all(f32[16,32,256]{2,1,0:T(8,128)S(1)} %stack.10), channel_id=1, replica_groups=mesh['row_0'=8,'row_1'=2,'col_0'=4,'col_1'=4] {'row_0','row_1'}, dimensions={0} | all-to-all | bytes 1048576 | tf_op jit(solution)/shard_map/all_to_all | solution.py:73
  227.7 9.7 %fusion.10 = f32[32,512]{1,0:T(8,128)S(1)} fusion(f32[32,4096]{1,0:T(8,128)S(1)} %bitcast.69, f32[512,4096]{1,0:T(8,128)} %param.6), kind=kOutput, calls=%fused_computation.32 | convolution fusion | flops 805306368 | bytes 8978432 | tf_op jit(solution)/shard_map/dot_general | solution.py:45
  237.6 20.2 %all_to_all.66 = f32[16,32,512]{2,1,0:T(8,128)S(1)} all-to-all(f32[16,32,512]{2,1,0:T(8,128)S(1)} %broadcast_in_dim.48), channel_id=1, replica_groups=mesh['row_0'=8,'row_1'=2,'col_0'=4,'col_1'=4] {'col_0','col_1'}, dimensions={0} | all-to-all | bytes 2097152 | tf_op jit(solution)/shard_map/all_to_all | solution.py:17
  257.8 9.9 %convolution_bitcast_fusion.1 = f32[16,32,256]{2,1,0:T(8,128)S(1)} fusion(f32[16,256,512]{2,1,0:T(8,128)} %bitcast.64, f32[32,512]{1,0:T(8,128)S(1)} %reduce_sum.133), kind=kOutput, calls=%fused_computation.1 | convolution fusion | flops 805306368 | bytes 8978432 | tf_op jit(solution)/shard_map/dot_general | solution.py:55
  267.7 19.2 %all_to_all.67 = f32[16,32,256]{2,1,0:T(8,128)S(1)} all-to-all(f32[16,32,256]{2,1,0:T(8,128)S(1)} %convolution_bitcast_fusion.1), channel_id=1, replica_groups=mesh['row_0'=8,'row_1'=2,'col_0'=4,'col_1'=4] {'row_0','row_1'}, dimensions={0} | all-to-all | bytes 1048576 | tf_op jit(solution)/shard_map/all_to_all | solution.py:34
  287.1 14.9 %all-reduce.1 = (f32[32,1]{0,1:T(1,128)S(1)}, f32[32,1]{0,1:T(1,128)S(1)}) all-reduce(f32[32,1]{0,1:T(1,128)S(1)} %bitcast.84, f32[32,1]{0,1:T(1,128)S(1)} %bitcast.83), channel_id=1, replica_groups=mesh['row_0'=8,'row_1'=2,'col_0'=4,'col_1'=4] {'row_0'}, use_global_device_ids=true, to_apply=%region_15.0 | all-reduce | flops 64 | bytes 512 | tf_op jit(solution)/shard_map/psum | solution.py:40
  313.0 9.2 %all-reduce.4 = (f32[32,1]{0,1:T(1,128)S(1)}, f32[32,1]{0,1:T(1,128)S(1)}) all-reduce(f32[32,1]{0,1:T(1,128)S(1)} %get-tuple-element.23, f32[32,1]{0,1:T(1,128)S(1)} %get-tuple-element.24), channel_id=1, replica_groups=mesh['row_0'=8,'row_1'=2,'col_0'=4,'col_1'=4] {'col_1'}, use_global_device_ids=true, to_apply=%region_18.0 | all-reduce | flops 64 | bytes 512 | tf_op jit(solution)/shard_map/psum | solution.py:40
  322.4 21.8 %all_to_all.68 = f32[16,32,256]{2,1,0:T(8,128)S(1)} all-to-all(f32[16,32,256]{2,1,0:T(8,128)S(1)} %stack.11), channel_id=1, replica_groups=mesh['row_0'=8,'row_1'=2,'col_0'=4,'col_1'=4] {'row_0','row_1'}, dimensions={0} | all-to-all | bytes 1048576 | tf_op jit(solution)/shard_map/all_to_all | solution.py:73
  344.2 9.7 %fusion.11 = f32[32,512]{1,0:T(8,128)S(1)} fusion(f32[32,4096]{1,0:T(8,128)S(1)} %bitcast.70, f32[512,4096]{1,0:T(8,128)} %param.6), kind=kOutput, calls=%fused_computation.33 | convolution fusion | flops 805306368 | bytes 8978432 | tf_op jit(solution)/shard_map/dot_general | solution.py:45
  354.1 20.5 %all_to_all.69 = f32[16,32,512]{2,1,0:T(8,128)S(1)} all-to-all(f32[16,32,512]{2,1,0:T(8,128)S(1)} %broadcast_in_dim.51), channel_id=1, replica_groups=mesh['row_0'=8,'row_1'=2,'col_0'=4,'col_1'=4] {'col_0','col_1'}, dimensions={0} | all-to-all | bytes 2097152 | tf_op jit(solution)/shard_map/all_to_all | solution.py:17
  374.7 10.7 %convolution_bitcast_fusion = f32[16,32,256]{2,1,0:T(8,128)} fusion(f32[16,256,512]{2,1,0:T(8,128)} %bitcast.65, f32[32,512]{1,0:T(8,128)S(1)} %reduce_sum.137), kind=kOutput, calls=%fused_computation | convolution fusion | flops 805306368 | bytes 8978432 | tf_op jit(solution)/shard_map/dot_general | solution.py:55
  389.0 15.9 %all-to-all-done.11 = f32[16,32,256]{2,1,0:T(8,128)S(1)} async-done(((f32[16,32,256]{2,1,0:T(8,128)}), f32[16,32,256]{2,1,0:T(8,128)S(1)}, u32[]{:S(2)}, u32[]{:S(2)}) %all-to-all-start.11) | async-done | bytes 524320 | tf_op jit(solution)/shard_map/all_to_all | solution.py:34
  405.0 15.0 %all-reduce = (f32[32,1]{0,1:T(1,128)S(1)}, f32[32,1]{0,1:T(1,128)S(1)}) all-reduce(f32[32,1]{0,1:T(1,128)S(1)} %bitcast.80, f32[32,1]{0,1:T(1,128)S(1)} %bitcast.79), channel_id=1, replica_groups=mesh['row_0'=8,'row_1'=2,'col_0'=4,'col_1'=4] {'row_0'}, use_global_device_ids=true, to_apply=%region_27.0 | all-reduce | flops 64 | bytes 512 | tf_op jit(solution)/shard_map/psum | solution.py:40
  431.0 9.2 %all-reduce.3 = (f32[32,1]{0,1:T(1,128)S(1)}, f32[32,1]{0,1:T(1,128)S(1)}) all-reduce(f32[32,1]{0,1:T(1,128)S(1)} %get-tuple-element.21, f32[32,1]{0,1:T(1,128)S(1)} %get-tuple-element.22), channel_id=1, replica_groups=mesh['row_0'=8,'row_1'=2,'col_0'=4,'col_1'=4] {'col_1'}, use_global_device_ids=true, to_apply=%region_30.0 | all-reduce | flops 64 | bytes 512 | tf_op jit(solution)/shard_map/psum | solution.py:40
  (54 shorter events, 70.5 us)
Async XLA Ops:
  0.6 59.3 %copy-start.2 = (f32[32,512]{1,0:T(8,128)S(1)}, f32[32,512]{1,0:T(8,128)}, u32[]{:S(2)}) copy-start(f32[32,512]{1,0:T(8,128)} %param.7) | copy-start | bytes 196612
  35.6 50.8 %copy-start = (f32[32,256]{1,0:T(8,128)S(1)}, f32[32,256]{1,0:T(8,128)}, u32[]{:S(2)}) copy-start(f32[32,256]{1,0:T(8,128)} %param.8) | copy-start | bytes 98308
  35.6 50.8 %copy-start.1 = (f32[32,256]{1,0:T(8,128)S(1)}, f32[32,256]{1,0:T(8,128)}, u32[]{:S(2)}) copy-start(f32[32,256]{1,0:T(8,128)} %param.10) | copy-start | bytes 98308
  35.6 50.8 %copy-start.3 = (f32[32,256]{1,0:T(8,128)S(1)}, f32[32,256]{1,0:T(8,128)}, u32[]{:S(2)}) copy-start(f32[32,256]{1,0:T(8,128)} %param.9) | copy-start | bytes 98308
  117.5 21.5 %all-to-all-start.4 = ((f32[16,32,512]{2,1,0:T(8,128)}), f32[16,32,512]{2,1,0:T(8,128)S(1)}, u32[]{:S(2)}, u32[]{:S(2)}) async-start(f32[16,32,512]{2,1,0:T(8,128)} %broadcast_in_dim.22), calls=%async_computation.4 | async-start | bytes 2097152 | tf_op jit(solution)/shard_map/all_to_all | solution.py:17
  354.0 35.0 %copy-start.4 = (f32[32]{0:T(128)S(1)}, f32[32]{0:T(128)}, u32[]{:S(2)}) copy-start(f32[32]{0:T(128)} %param.11) | copy-start | bytes 388
  385.4 19.5 %all-to-all-start.11 = ((f32[16,32,256]{2,1,0:T(8,128)}), f32[16,32,256]{2,1,0:T(8,128)S(1)}, u32[]{:S(2)}, u32[]{:S(2)}) async-start(f32[16,32,256]{2,1,0:T(8,128)} %convolution_bitcast_fusion), calls=%async_computation.11 | async-start | bytes 1048576 | tf_op jit(solution)/shard_map/all_to_all | solution.py:34
